TPU v7x, 32 devices: a whole 2x2x4 slice. The times are simulated.
32 devices in a mesh: comp: 8 (over z, core), blk: 4 (over y, x).
Axes of the slice: x: 2, y: 2, z: 4, core: 2. Of those that a mesh axis runs over, the one named last changes fastest.
Arguments:
- state_now: float32 [8, 6, 32, 32, 256], P('comp', None, 'blk'), may hold values from -5 to 5
- state_prev: float32 [8, 6, 32, 32, 256], P('comp', None, 'blk'), may hold values from -5 to 5
- viscosity: float32 [8, 32, 32, 256], P('comp', 'blk'), may hold values from 0.05 to 0.5
- jacobian: float32 [8, 3, 6, 6], P('comp'), may hold values from -0.4 to 0.4
- donor_cell: int32 [8, 4, 8, 2, 8, 128], P('comp', 'blk'), may hold values from 0 to 57343, as said below
- interp_weight: float32 [8, 4, 8, 2, 8, 128], P('comp', 'blk'), may hold values from 0 to 1
- recv_cell: int32 [8, 4, 8, 2, 128], P('comp', 'blk'), may hold values from 0 to 57343, as said below
- pair_tiles: int32 [4, 8, 8], P('blk'), may hold values from 0 to 2, as said below
Outputs:
- state_next: float32 [8, 6, 32, 32, 256], P('comp', None, 'blk')
Inputs may be any that keep to these rules, and one draw needn't show every extreme that they name: `donor_cell`: the cells of one donor tile point are the eight corners of a cube of adjacent cells, corner k = 4 i + 2 j + l offset by (i, j, l). `recv_cell`: the receiving cells of one device are all different. `pair_tiles`: for each block index some destination component takes 2 tiles from every source component.
All inputs are finite; a program needn't handle non-finite values.
Results may differ from a plain program's by a relative error of at most 0.0003.
Values sent between devices are 32-bit elements; how exact they have to be, the bound alone decides.
A program may use at most 128 MiB of HBM per device.

v0:
```python
import functools

import jax
import jax.numpy as jnp
from jax import lax
from jax.experimental import pallas as pl
from jax.experimental.pallas import tpu as pltpu
from jax.sharding import PartitionSpec as P

SUBITERS = 2


time_scale = 0.5
pseudo_diag = 2.5

MESH = pl.DeviceIdType.MESH
VMEM_LIMIT = 60 * 1024 * 1024
F32 = jnp.float32
BF16 = jnp.bfloat16


def split(value):
    high = value.astype(BF16)
    low = (value - high.astype(F32)).astype(BF16)
    return high, low


def fill_mix(jac_ref, mix_hi, mix_lo, nvar, width_y):
    columns = mix_hi.shape[1]
    row = lax.broadcasted_iota(jnp.int32, (width_y, columns), 0)
    col = lax.broadcasted_iota(jnp.int32, (width_y, columns), 1)
    for v in range(nvar):
        block = jnp.zeros((width_y, columns), F32)
        for d in range(3):
            for w in range(nvar):
                block = jnp.where(col == row + (d * nvar + w) * width_y, 0.5 * jac_ref[d, v, w], block)
        high, low = split(block)
        mix_hi[v * width_y : (v + 1) * width_y, :] = high
        mix_lo[v * width_y : (v + 1) * width_y, :] = low


def flux_plane(centre, below, above, kappa, mix_hi, mix_lo):
    shape = centre.shape
    nvar, width_y, width_z = shape
    flat = centre.reshape(nvar * width_y, width_z)
    at_y = lax.broadcasted_iota(jnp.int32, shape, 1)
    at_z = lax.broadcasted_iota(jnp.int32, shape, 2)

    def moved(shift, axis, keep):
        return jnp.where(keep, pltpu.roll(flat, shift, axis).reshape(shape), 0.0)

    next_y = moved(nvar * width_y - 1, 0, at_y < width_y - 1)
    last_y = moved(1, 0, at_y > 0)
    next_z = moved(width_z - 1, 1, at_z < width_z - 1)
    last_z = moved(1, 1, at_z > 0)
    beside = (above + below) + (next_y + last_y) + (next_z + last_z)
    diffs = [above - below, next_y - last_y, next_z - last_z]
    diffs = jnp.concatenate([d.reshape(flat.shape) for d in diffs], axis=0)
    high, low = split(diffs)
    hi = mix_hi[...]
    convect = jnp.dot(hi, high, preferred_element_type=F32)
    convect += jnp.dot(mix_lo[...], high, preferred_element_type=F32)
    convect += jnp.dot(hi, low, preferred_element_type=F32)
    return convect.reshape(shape) + kappa[None] * (6.0 * centre - beside)


def relax_kernel(
    count, jac_ref, state_ref, now_ref, prev_ref, kappa_ref, out_ref,
    halo, rstar, first, second, mix_hi, mix_lo, send_sem, recv_sem,
):
    me = lax.axis_index("blk")
    right = lax.rem(me + 1, count)
    left = lax.rem(me + count - 1, count)
    has_left = me > 0
    has_right = me < count - 1
    nvar, rows, width_y, width_z = state_ref.shape
    barrier = pltpu.get_barrier_semaphore()

    @pl.when(has_left)
    def _():
        pl.semaphore_signal(barrier, inc=1, device_id={"blk": left}, device_id_type=MESH)

    @pl.when(has_right)
    def _():
        pl.semaphore_signal(barrier, inc=1, device_id={"blk": right}, device_id_type=MESH)

    @pl.when(jnp.logical_not(has_left))
    def _():
        for k in range(3):
            halo[k, 0] = jnp.zeros((nvar, width_y, width_z), F32)

    @pl.when(jnp.logical_not(has_right))
    def _():
        for k in range(3):
            halo[k, 1] = jnp.zeros((nvar, width_y, width_z), F32)

    pl.semaphore_wait(barrier, has_left.astype(jnp.int32) + has_right.astype(jnp.int32))

    fields = [state_ref, first, second]

    def to_left(k):
        return pltpu.make_async_remote_copy(
            src_ref=fields[k].at[:, 0], dst_ref=halo.at[k, 1],
            send_sem=send_sem.at[k, 1], recv_sem=recv_sem.at[k, 1],
            device_id={"blk": left}, device_id_type=MESH,
        )

    def to_right(k):
        return pltpu.make_async_remote_copy(
            src_ref=fields[k].at[:, rows - 1], dst_ref=halo.at[k, 0],
            send_sem=send_sem.at[k, 0], recv_sem=recv_sem.at[k, 0],
            device_id={"blk": right}, device_id_type=MESH,
        )

    def start(k):
        @pl.when(has_left)
        def _():
            to_left(k).start()

        @pl.when(has_right)
        def _():
            to_right(k).start()

    def arrive(k):
        @pl.when(has_left)
        def _():
            to_right(k).wait_recv()

        @pl.when(has_right)
        def _():
            to_left(k).wait_recv()

    def plane(k, x, below, above):
        kappa = kappa_ref[x]
        centre = fields[k][:, x]
        flow = flux_plane(centre, below, above, kappa, mix_hi, mix_lo)
        scale = -1.0 / (pseudo_diag + 6.0 * kappa)
        if k == 0:
            base = time_scale * (3.0 * centre - 4.0 * now_ref[:, x] + prev_ref[:, x]) + flow
            rstar[:, x] = base
            first[:, x] = base * scale[None]
        else:
            step = (rstar[:, x] + flow - 6.0 * kappa[None] * centre) * scale[None]
            if k == 1:
                second[:, x] = step
            else:
                out_ref[:, x] = state_ref[:, x] + step

    start(0)
    fill_mix(jac_ref, mix_hi, mix_lo, nvar, width_y)
    for k in range(3):
        field = fields[k]

        def inner(x, carry, k=k, field=field):
            plane(k, x, field[:, x - 1], field[:, x + 1])
            return carry

        lax.fori_loop(1, rows - 1, inner, 0)
        arrive(k)
        plane(k, 0, halo[k, 0], field[:, 1])
        plane(k, rows - 1, field[:, rows - 2], halo[k, 1])
        if k < 2:
            start(k + 1)
    for k in range(3):
        @pl.when(has_left)
        def _(k=k):
            to_left(k).wait_send()

        @pl.when(has_right)
        def _(k=k):
            to_right(k).wait_send()


def relax(jac, state, now, prev, kappa):
    count = lax.axis_size("blk")
    nvar, rows, width_y, width_z = state.shape
    vmem = pl.BlockSpec(memory_space=pltpu.VMEM)
    whole = pltpu.VMEM(state.shape, F32)
    mixed = pltpu.VMEM((nvar * width_y, 3 * nvar * width_y), BF16)
    return pl.pallas_call(
        functools.partial(relax_kernel, count),
        out_shape=jax.ShapeDtypeStruct(state.shape, F32),
        in_specs=[pl.BlockSpec(memory_space=pltpu.SMEM)] + [vmem] * 4,
        out_specs=vmem,
        scratch_shapes=[
            pltpu.VMEM((3, 2, nvar, width_y, width_z), F32),
            whole, whole, whole, mixed, mixed,
            pltpu.SemaphoreType.DMA((3, 2)),
            pltpu.SemaphoreType.DMA((3, 2)),
        ],
        compiler_params=pltpu.CompilerParams(
            collective_id=0, has_side_effects=True, vmem_limit_bytes=VMEM_LIMIT
        ),
        name="relax",
    )(jac, state, now, prev, kappa)


def gather_kernel(strides, live_ref, state_ref, base_ref, weight_ref, out_ref, packed):
    nvar, pairs, width_z = state_ref.shape
    width_y, shift = strides
    tiles, _, tile = base_ref.shape
    for v in range(nvar):
        high, low = split(state_ref[v])
        packed[v * pairs : (v + 1) * pairs, :width_z] = high
        packed[v * pairs : (v + 1) * pairs, width_z:] = low

    def one(t, carry):
        @pl.when(live_ref[t] > 0)
        def _():
            base = base_ref[t]
            pair = lax.shift_right_logical(base, shift)
            depth = jnp.bitwise_and(base, width_z - 1)
            depth = jnp.concatenate([depth, depth + 1], axis=1)
            pair = jnp.concatenate([pair, pair], axis=1)
            at_z = lax.broadcasted_iota(jnp.int32, (width_z, 2 * tile), 0)
            hot = jnp.where(at_z == depth, 1.0, 0.0).astype(BF16)
            hot = jnp.concatenate([hot, hot], axis=0)
            found = jnp.dot(packed[...], hot, preferred_element_type=F32)
            at_pair = lax.broadcasted_iota(jnp.int32, (pairs, 2 * tile), 0) - pair
            weights = weight_ref[t]
            spread = jnp.zeros((pairs, 2 * tile), F32)
            for i in range(2):
                for j in range(2):
                    k = 4 * i + 2 * j
                    row = jnp.concatenate([weights[k : k + 1], weights[k + 1 : k + 2]], axis=1)
                    spread = jnp.where(at_pair == i * width_y + j, row, spread)
            total = (found.reshape(nvar, pairs, 2 * tile) * spread[None]).sum(axis=1)
            out_ref[t] = total[:, :tile] + total[:, tile:]

        @pl.when(live_ref[t] <= 0)
        def _():
            out_ref[t] = jnp.zeros((nvar, tile), F32)

        return carry

    lax.fori_loop(0, tiles, one, 0)


def gather(live, state, base, weights):
    nvar, rows, width_y, width_z = state.shape
    pairs = rows * width_y
    tiles, _, tile = base.shape
    vmem = pl.BlockSpec(memory_space=pltpu.VMEM)
    return pl.pallas_call(
        functools.partial(gather_kernel, (width_y, width_z.bit_length() - 1)),
        out_shape=jax.ShapeDtypeStruct((tiles, nvar, tile), F32),
        in_specs=[pl.BlockSpec(memory_space=pltpu.SMEM)] + [vmem] * 3,
        out_specs=vmem,
        scratch_shapes=[pltpu.VMEM((nvar * pairs, 2 * width_z), BF16)],
        compiler_params=pltpu.CompilerParams(vmem_limit_bytes=VMEM_LIMIT),
        name="gather",
    )(live, state.reshape(nvar, pairs, width_z), base, weights)


def scatter_kernel(shift, state_ref, cell_ref, value_ref, out_ref, rows_ref, total):
    nvar, pairs, width_z = state_ref.shape
    tiles, _, tile = cell_ref.shape
    total[...] = jnp.zeros_like(total)
    rows_ref[nvar * pairs :, tile:] = jnp.zeros((pairs, tile), BF16)

    def one(t, carry):
        cell = cell_ref[t]
        pair = lax.shift_right_arithmetic(cell, shift)
        depth = jnp.bitwise_and(cell, width_z - 1)
        hot = lax.broadcasted_iota(jnp.int32, (width_z, tile), 0) == depth
        hot = jnp.where(hot, 1.0, 0.0).astype(BF16)
        hot = jnp.concatenate([hot, hot], axis=1)
        here = lax.broadcasted_iota(jnp.int32, (pairs, tile), 0) == pair
        values = value_ref[t]
        high = values.astype(BF16).astype(F32)
        low = values - high
        for v in range(nvar):
            at = slice(v * pairs, (v + 1) * pairs)
            rows_ref[at, :tile] = jnp.where(here, high[v : v + 1], 0.0).astype(BF16)
            rows_ref[at, tile:] = jnp.where(here, low[v : v + 1], 0.0).astype(BF16)
        rows_ref[nvar * pairs :, :tile] = jnp.where(here, 1.0, 0.0).astype(BF16)
        total[...] += lax.dot_general(
            rows_ref[...], hot, (((1,), (1,)), ((), ())), preferred_element_type=F32
        )
        return carry

    lax.fori_loop(0, tiles, one, 0)
    hit = total[nvar * pairs :, :] > 0.5
    for v in range(nvar):
        out_ref[v] = jnp.where(hit, total[v * pairs : (v + 1) * pairs, :], state_ref[v])


def scatter(state, cells, values):
    nvar, rows, width_y, width_z = state.shape
    pairs = rows * width_y
    tile = cells.shape[2]
    vmem = pl.BlockSpec(memory_space=pltpu.VMEM)
    out = pl.pallas_call(
        functools.partial(scatter_kernel, width_z.bit_length() - 1),
        out_shape=jax.ShapeDtypeStruct((nvar, pairs, width_z), F32),
        in_specs=[vmem] * 3,
        out_specs=vmem,
        scratch_shapes=[
            pltpu.VMEM(((nvar + 1) * pairs, 2 * tile), BF16),
            pltpu.VMEM(((nvar + 1) * pairs, width_z), F32),
        ],
        compiler_params=pltpu.CompilerParams(vmem_limit_bytes=VMEM_LIMIT),
        name="scatter",
    )(state.reshape(nvar, pairs, width_z), cells, values)
    return out.reshape(state.shape)


def shards(
    state_now, state_prev, viscosity, jacobian, donor_cell, interp_weight, recv_cell, pair_tiles
):
    now = state_now[0]
    prev = state_prev[0]
    kappa = viscosity[0]
    jac = jacobian[0]
    nvar = now.shape[0]
    comps = lax.axis_size("comp")
    mine = lax.axis_index("comp")
    slots, corners, tile = donor_cell.shape[3:]
    tiles = comps * slots
    slot = jnp.arange(slots, dtype=jnp.int32)[None, :]
    live_in = lax.dynamic_index_in_dim(pair_tiles[0], mine, 1, keepdims=False)
    live_out = lax.dynamic_index_in_dim(pair_tiles[0], mine, 0, keepdims=False)
    keep = (slot < live_in[:, None]).reshape(tiles, 1, 1)
    cells = jnp.where(keep, recv_cell[0, 0].reshape(tiles, 1, tile), -1)
    send = (slot < live_out[:, None]).astype(jnp.int32).reshape(tiles)
    base = donor_cell[0, 0].reshape(tiles, corners, tile)[:, :1]
    held = lax.all_to_all(interp_weight[0, 0], "comp", split_axis=0, concat_axis=0, tiled=True)
    held = held.reshape(tiles, corners, tile)
    state = now
    for sub in range(SUBITERS):
        state = relax(jac, state, now, prev, kappa)
        packed = gather(send, state, base, held)
        packed = packed.reshape(comps, slots * nvar, tile)
        arrived = lax.all_to_all(packed, "comp", split_axis=0, concat_axis=0, tiled=True)
        state = scatter(state, cells, arrived.reshape(tiles, nvar, tile))
    return state[None]


def solution(mesh):
    in_specs = (
        P("comp", None, "blk", None, None),
        P("comp", None, "blk", None, None),
        P("comp", "blk", None, None),
        P("comp", None, None, None),
        P("comp", "blk", None, None, None, None),
        P("comp", "blk", None, None, None, None),
        P("comp", "blk", None, None, None),
        P("blk", None, None),
    )
    out_specs = P("comp", None, "blk", None, None)
    return jax.shard_map(shards, mesh=mesh, in_specs=in_specs, out_specs=out_specs, check_vma=False)
```

profile of v0, /device:TPU:6, one launch (start us, length us, event | category | flops | bytes accessed | tf_op | source)
XLA Modules:
  0.0 136.8 jit_solution(3479975213249578941)
XLA Ops:
  0.0 0.0 copy-start
  0.0 5.0 %all-to-all-start = ((f32[8,2,8,128]{3,2,1,0:T(8,128)}), f32[8,2,8,128]{3,2,1,0:T(8,128)S(1)}, u32[]{:S(2)}, u32[]{:S(2)}) async-start(f32[8,2,8,128]{3,2,1,0:T(8,128)} %bitcast.32), calls=%async_computation | async-start | bytes 131072 | tf_op jit(solution)/shard_map/all_to_all | solution.py:327
  5.0 0.0 copy-done
  5.0 0.2 dynamic-slice_reduce_fusion
  5.2 0.1 iota_compare_fusion.1
  5.3 0.1 lt.50
  5.4 0.1 fusion
  5.5 0.6 reshape.94.live_ref
  6.1 1.4 %slice.4.base_ref = s32[16,1,128]{2,1,0:T(1,128)} slice(s32[16,8,128]{2,1,0:T(8,128)} %bitcast.34), slice={[0:16], [0:1], [0:128]} | slice | bytes 16384 | tf_op jit(solution)/shard_map/slice | solution.py:326
  7.5 1.3 copy.11
  8.8 35.8 %relax.2 = f32[6,8,32,256]{3,2,1,0:T(8,128)} custom-call(f32[3,6,6]{2,1,0:T(8,128)} %bitcast.30, f32[6,8,32,256]{3,2,1,0:T(8,128)} %bitcast.20, f32[6,8,32,256]{3,2,1,0:T(8,128)} %bitcast.21, f32[6,8,32,256]{3,2,1,0:T(8,128)} %bitcast.24, f32[8,32,256]{2,1,0:T(8,128)} %bitcast.26), custom_call_target="tpu_custom_call" | custom-call | tf_op jit(solution)/shard_map/relax/pallas_call | solution.py:180
  44.6 0.0 copy-start.2
  44.6 0.0 all-to-all-done
  44.6 0.0 copy-start.1
  44.6 0.6 copy-done.1
  45.2 7.8 %gather.2 = f32[16,6,128]{2,1,0:T(8,128)} custom-call(s32[16]{0:T(128)} %reshape.94.live_ref, f32[6,256,256]{2,1,0:T(8,128)} %bitcast.16, s32[16,1,128]{2,1,0:T(1,128)} %slice.4.base_ref, f32[16,8,128]{2,1,0:T(8,128)} %bitcast.28), custom_call_target="tpu_custom_call" | custom-call | tf_op jit(solution)/shard_map/gather/pallas_call | solution.py:244
  53.1 1.5 %reshape.88 = f32[8,12,128]{2,1,0:T(8,128)} reshape(f32[16,6,128]{2,1,0:T(8,128)} %gather.2) | data formatting | bytes 98304 | tf_op jit(solution)/shard_map/reshape | solution.py:333
  54.6 4.9 %all-to-all-start.1 = ((f32[8,12,128]{2,1,0:T(8,128)}), f32[8,12,128]{2,1,0:T(8,128)S(1)}, u32[]{:S(2)}, u32[]{:S(2)}) async-start(f32[8,12,128]{2,1,0:T(8,128)} %reshape.88), calls=%async_computation.1 | async-start | bytes 131072 | tf_op jit(solution)/shard_map/all_to_all | solution.py:334
  59.5 0.0 copy-done.2
  59.5 0.7 broadcast_select_fusion.cell_ref
  60.1 5.2 %all-to-all-done.1 = f32[8,12,128]{2,1,0:T(8,128)S(1)} async-done(((f32[8,12,128]{2,1,0:T(8,128)}), f32[8,12,128]{2,1,0:T(8,128)S(1)}, u32[]{:S(2)}, u32[]{:S(2)}) %all-to-all-start.1) | async-done | bytes 49184 | tf_op jit(solution)/shard_map/all_to_all | solution.py:334
  65.4 0.6 reshape.89.value_ref
  66.0 10.1 %scatter.2 = f32[6,256,256]{2,1,0:T(8,128)} custom-call(f32[6,256,256]{2,1,0:T(8,128)} %bitcast.17, s32[16,1,128]{2,1,0:T(1,128)} %broadcast_select_fusion.cell_ref, f32[16,6,128]{2,1,0:T(8,128)} %reshape.89.value_ref), custom_call_target="tpu_custom_call" | custom-call | tf_op jit(solution)/shard_map/scatter/pallas_call | solution.py:293
  76.2 32.5 %relax.3 = f32[6,8,32,256]{3,2,1,0:T(8,128)} custom-call(f32[3,6,6]{2,1,0:T(8,128)} %bitcast.31, f32[6,8,32,256]{3,2,1,0:T(8,128)} %bitcast.23, f32[6,8,32,256]{3,2,1,0:T(8,128)} %bitcast.22, f32[6,8,32,256]{3,2,1,0:T(8,128)} %bitcast.25, f32[8,32,256]{2,1,0:T(8,128)} %bitcast.27), custom_call_target="tpu_custom_call" | custom-call | tf_op jit(solution)/shard_map/relax/pallas_call | solution.py:180
  108.7 7.8 %gather.3 = f32[16,6,128]{2,1,0:T(8,128)} custom-call(s32[16]{0:T(128)} %reshape.94.live_ref, f32[6,256,256]{2,1,0:T(8,128)} %bitcast.18, s32[16,1,128]{2,1,0:T(1,128)} %slice.4.base_ref, f32[16,8,128]{2,1,0:T(8,128)} %bitcast.29), custom_call_target="tpu_custom_call" | custom-call | tf_op jit(solution)/shard_map/gather/pallas_call | solution.py:244
  116.5 0.8 reshape.92
  117.4 8.6 %all_to_all.15 = f32[8,12,128]{2,1,0:T(8,128)S(1)} all-to-all(f32[8,12,128]{2,1,0:T(8,128)S(1)} %reshape.92), channel_id=1, replica_groups=mesh['comp'=8,'blk'=4] {'comp'}, dimensions={0} | all-to-all | bytes 98304 | tf_op jit(solution)/shard_map/all_to_all | solution.py:334
  126.0 0.6 reshape.93.value_ref
  126.6 10.2 %scatter.3 = f32[6,256,256]{2,1,0:T(8,128)} custom-call(f32[6,256,256]{2,1,0:T(8,128)} %bitcast.19, s32[16,1,128]{2,1,0:T(1,128)} %broadcast_select_fusion.cell_ref, f32[16,6,128]{2,1,0:T(8,128)} %reshape.93.value_ref), custom_call_target="tpu_custom_call" | custom-call | tf_op jit(solution)/shard_map/scatter/pallas_call | solution.py:293
  (1 shorter events, 0.0 us)
Async XLA Ops:
  0.0 5.0 %copy-start = (s32[1,8,8]{2,1,0:T(8,128)S(1)}, s32[1,8,8]{2,1,0:T(8,128)}, u32[]{:S(2)}) copy-start(s32[1,8,8]{2,1,0:T(8,128)} %param.15) | copy-start | bytes 772
  0.0 44.6 %all-to-all-start = ((f32[8,2,8,128]{3,2,1,0:T(8,128)}), f32[8,2,8,128]{3,2,1,0:T(8,128)S(1)}, u32[]{:S(2)}, u32[]{:S(2)}) async-start(f32[8,2,8,128]{3,2,1,0:T(8,128)} %bitcast.32), calls=%async_computation | async-start | bytes 131072 | tf_op jit(solution)/shard_map/all_to_all | solution.py:327
  44.6 14.9 %copy-start.2 = (s32[1,1,8,2,128]{4,3,2,1,0:T(2,128)S(1)}, s32[1,1,8,2,128]{4,3,2,1,0:T(2,128)}, u32[]{:S(2)}) copy-start(s32[1,1,8,2,128]{4,3,2,1,0:T(2,128)} %param.14) | copy-start | bytes 24580
  44.6 0.6 copy-start.1
  54.6 10.8 %all-to-all-start.1 = ((f32[8,12,128]{2,1,0:T(8,128)}), f32[8,12,128]{2,1,0:T(8,128)S(1)}, u32[]{:S(2)}, u32[]{:S(2)}) async-start(f32[8,12,128]{2,1,0:T(8,128)} %reshape.88), calls=%async_computation.1 | async-start | bytes 131072 | tf_op jit(solution)/shard_map/all_to_all | solution.py:334
where the time goes:
time: 138 us; the launch traced here: 137 us
  Pallas kernels  104 us (75%)
  starting transfers between devices  9.92 us (7%)
  blocking collectives  8.61 us (6%)
  local copies, waits for them, and re-layouts  7.82 us (6%)
  waiting for transfers between devices  5.24 us (4%)
    pallas_call x2, Pallas kernels, relax(): pl.pallas_call(functools.partial(relax_kernel, count), out_shape=jax.Shap...  68.3 us
    pallas_call x2, Pallas kernels, scatter(): pl.pallas_call(functools.partial(scatter_kernel, width_z.bit_length() - 1...  20.3 us
    pallas_call x2, Pallas kernels, gather(): pl.pallas_call(functools.partial(gather_kernel, (width_y, width_z.bit_len...  15.7 us
    all_to_all x1, blocking collectives, shards(): lax.all_to_all(packed, 'comp', split_axis=0, concat_axis=0, tiled=True)  8.61 us
    all_to_all x1, waiting for transfers between devices, shards(): lax.all_to_all(packed, 'comp', split_axis=0, concat_axis=0, tiled=True)  5.23 us
    all_to_all x1, starting transfers between devices, shards(): lax.all_to_all(interp_weight[0, 0], 'comp', split_axis=0, concat_axis=0,...  5.01 us
    all_to_all x1, starting transfers between devices, shards(): lax.all_to_all(packed, 'comp', split_axis=0, concat_axis=0, tiled=True)  4.91 us
  transfers between devices with their start and end apart: 2, of which 1 were waited for; matrix products, arithmetic and copies ran while one was open for 3% of the time, Pallas kernels for 26%

commit v1 on v0

--- a/solution.py
+++ b/solution.py
@@ -64,10 +64,36 @@
     return convect.reshape(shape) + kappa[None] * (6.0 * centre - beside)
 
 
-def relax_kernel(
-    count, jac_ref, state_ref, now_ref, prev_ref, kappa_ref, out_ref,
-    halo, rstar, first, second, mix_hi, mix_lo, send_sem, recv_sem,
-):
+def comp_copies(comps, source_ref, landing, send_sem, recv_sem):
+    mine = lax.axis_index("comp")
+
+    def copy(d):
+        peer = lax.rem(mine + d, comps)
+        return pltpu.make_async_remote_copy(
+            src_ref=source_ref.at[peer], dst_ref=landing.at[d],
+            send_sem=send_sem.at[d], recv_sem=recv_sem.at[d],
+            device_id={"comp": peer}, device_id_type=MESH,
+        )
+
+    return mine, copy
+
+
+def greet_comps(comps, barrier):
+    mine = lax.axis_index("comp")
+    for d in range(1, comps):
+        peer = lax.rem(mine + d, comps)
+        pl.semaphore_signal(barrier, inc=1, device_id={"comp": peer}, device_id_type=MESH)
+
+
+def relax_kernel(count, comps, jac_ref, state_ref, now_ref, prev_ref, kappa_ref, *refs):
+    if comps:
+        weight_ref, out_ref, held_ref = refs[:3]
+        landing, weight_send, weight_recv = refs[-3:]
+        refs = refs[3:-3]
+    else:
+        out_ref = refs[0]
+        refs = refs[1:]
+    halo, rstar, first, second, mix_hi, mix_lo, send_sem, recv_sem = refs
     me = lax.axis_index("blk")
     right = lax.rem(me + 1, count)
     left = lax.rem(me + count - 1, count)
@@ -84,6 +110,9 @@
     def _():
         pl.semaphore_signal(barrier, inc=1, device_id={"blk": right}, device_id_type=MESH)
 
+    if comps:
+        greet_comps(comps, barrier)
+
     @pl.when(jnp.logical_not(has_left))
     def _():
         for k in range(3):
@@ -94,7 +123,8 @@
         for k in range(3):
             halo[k, 1] = jnp.zeros((nvar, width_y, width_z), F32)
 
-    pl.semaphore_wait(barrier, has_left.astype(jnp.int32) + has_right.astype(jnp.int32))
+    peers = has_left.astype(jnp.int32) + has_right.astype(jnp.int32)
+    pl.semaphore_wait(barrier, peers + max(comps - 1, 0))
 
     fields = [state_ref, first, second]
 
@@ -147,6 +177,11 @@
                 out_ref[:, x] = state_ref[:, x] + step
 
     start(0)
+    if comps:
+        mine, copy = comp_copies(comps, weight_ref, landing, weight_send, weight_recv)
+        for d in range(1, comps):
+            copy(d).start()
+        held_ref[mine] = weight_ref[mine]
     fill_mix(jac_ref, mix_hi, mix_lo, nvar, width_y)
     for k in range(3):
         field = fields[k]
@@ -161,6 +196,10 @@
         plane(k, rows - 1, field[:, rows - 2], halo[k, 1])
         if k < 2:
             start(k + 1)
+    if comps:
+        for d in range(1, comps):
+            copy(d).wait()
+            held_ref[lax.rem(mine - d + comps, comps)] = landing[d]
     for k in range(3):
         @pl.when(has_left)
         def _(k=k):
@@ -171,28 +210,41 @@
             to_right(k).wait_send()
 
 
-def relax(jac, state, now, prev, kappa):
+def relax(jac, state, now, prev, kappa, weights=None):
     count = lax.axis_size("blk")
     nvar, rows, width_y, width_z = state.shape
     vmem = pl.BlockSpec(memory_space=pltpu.VMEM)
     whole = pltpu.VMEM(state.shape, F32)
     mixed = pltpu.VMEM((nvar * width_y, 3 * nvar * width_y), BF16)
+    operands = [jac, state, now, prev, kappa]
+    outs = [jax.ShapeDtypeStruct(state.shape, F32)]
+    scratch = [
+        pltpu.VMEM((3, 2, nvar, width_y, width_z), F32),
+        whole, whole, whole, mixed, mixed,
+        pltpu.SemaphoreType.DMA((3, 2)),
+        pltpu.SemaphoreType.DMA((3, 2)),
+    ]
+    comps = 0
+    if weights is not None:
+        comps = weights.shape[0]
+        operands.append(weights)
+        outs.append(jax.ShapeDtypeStruct(weights.shape, F32))
+        scratch += [
+            pltpu.VMEM(weights.shape, F32),
+            pltpu.SemaphoreType.DMA((comps,)),
+            pltpu.SemaphoreType.DMA((comps,)),
+        ]
     return pl.pallas_call(
-        functools.partial(relax_kernel, count),
-        out_shape=jax.ShapeDtypeStruct(state.shape, F32),
-        in_specs=[pl.BlockSpec(memory_space=pltpu.SMEM)] + [vmem] * 4,
-        out_specs=vmem,
-        scratch_shapes=[
-            pltpu.VMEM((3, 2, nvar, width_y, width_z), F32),
-            whole, whole, whole, mixed, mixed,
-            pltpu.SemaphoreType.DMA((3, 2)),
-            pltpu.SemaphoreType.DMA((3, 2)),
-        ],
+        functools.partial(relax_kernel, count, comps),
+        out_shape=outs,
+        in_specs=[pl.BlockSpec(memory_space=pltpu.SMEM)] + [vmem] * (len(operands) - 1),
+        out_specs=[vmem] * len(outs),
+        scratch_shapes=scratch,
         compiler_params=pltpu.CompilerParams(
-            collective_id=0, has_side_effects=True, vmem_limit_bytes=VMEM_LIMIT
+            collective_id=0 if comps else 1, has_side_effects=True, vmem_limit_bytes=VMEM_LIMIT
         ),
         name="relax",
-    )(jac, state, now, prev, kappa)
+    )(*operands)
 
 
 def gather_kernel(strides, live_ref, state_ref, base_ref, weight_ref, out_ref, packed):
@@ -252,54 +304,91 @@
     )(live, state.reshape(nvar, pairs, width_z), base, weights)
 
 
-def scatter_kernel(shift, state_ref, cell_ref, value_ref, out_ref, rows_ref, total):
+def scatter_kernel(
+    comps, shift, state_ref, cell_ref, value_ref, out_ref,
+    rows_ref, total, landing, send_sem, recv_sem,
+):
     nvar, pairs, width_z = state_ref.shape
-    tiles, _, tile = cell_ref.shape
-    total[...] = jnp.zeros_like(total)
-    rows_ref[nvar * pairs :, tile:] = jnp.zeros((pairs, tile), BF16)
-
-    def one(t, carry):
-        cell = cell_ref[t]
-        pair = lax.shift_right_arithmetic(cell, shift)
-        depth = jnp.bitwise_and(cell, width_z - 1)
-        hot = lax.broadcasted_iota(jnp.int32, (width_z, tile), 0) == depth
-        hot = jnp.where(hot, 1.0, 0.0).astype(BF16)
-        hot = jnp.concatenate([hot, hot], axis=1)
-        here = lax.broadcasted_iota(jnp.int32, (pairs, tile), 0) == pair
-        values = value_ref[t]
-        high = values.astype(BF16).astype(F32)
-        low = values - high
-        for v in range(nvar):
-            at = slice(v * pairs, (v + 1) * pairs)
-            rows_ref[at, :tile] = jnp.where(here, high[v : v + 1], 0.0).astype(BF16)
-            rows_ref[at, tile:] = jnp.where(here, low[v : v + 1], 0.0).astype(BF16)
-        rows_ref[nvar * pairs :, :tile] = jnp.where(here, 1.0, 0.0).astype(BF16)
-        total[...] += lax.dot_general(
-            rows_ref[...], hot, (((1,), (1,)), ((), ())), preferred_element_type=F32
+    slots, tile = cell_ref.shape[1], cell_ref.shape[3]
+    barrier = pltpu.get_barrier_semaphore()
+    greet_comps(comps, barrier)
+    mine, copy = comp_copies(comps, value_ref, landing, send_sem, recv_sem)
+    pl.semaphore_wait(barrier, comps - 1)
+    for d in range(1, comps):
+        copy(d).start()
+    landing[0] = value_ref[mine]
+    for s in range(slots):
+        low_at = slice((2 * s + 1) * tile, (2 * s + 2) * tile)
+        rows_ref[nvar * pairs :, low_at] = jnp.zeros((pairs, tile), BF16)
+
+    def one(d, carry):
+        @pl.when(d > 0)
+        def _():
+            copy(d).wait_recv()
+
+        source = lax.rem(mine - d + comps, comps)
+        hots = []
+        for s in range(slots):
+            cell = cell_ref[source, s]
+            pair = lax.shift_right_arithmetic(cell, shift)
+            depth = jnp.bitwise_and(cell, width_z - 1)
+            hot = lax.broadcasted_iota(jnp.int32, (width_z, tile), 0) == depth
+            hot = jnp.where(hot, 1.0, 0.0).astype(BF16)
+            hots += [hot, hot]
+            here = lax.broadcasted_iota(jnp.int32, (pairs, tile), 0) == pair
+            values = landing[d, s]
+            high = values.astype(BF16).astype(F32)
+            low = values - high
+            high_at = slice(2 * s * tile, (2 * s + 1) * tile)
+            low_at = slice((2 * s + 1) * tile, (2 * s + 2) * tile)
+            for v in range(nvar):
+                at = slice(v * pairs, (v + 1) * pairs)
+                rows_ref[at, high_at] = jnp.where(here, high[v : v + 1], 0.0).astype(BF16)
+                rows_ref[at, low_at] = jnp.where(here, low[v : v + 1], 0.0).astype(BF16)
+            rows_ref[nvar * pairs :, high_at] = jnp.where(here, 1.0, 0.0).astype(BF16)
+        part = lax.dot_general(
+            rows_ref[...], jnp.concatenate(hots, axis=1), (((1,), (1,)), ((), ())),
+            preferred_element_type=F32,
         )
+
+        @pl.when(d == 0)
+        def _():
+            total[...] = part
+
+        @pl.when(d > 0)
+        def _():
+            total[...] += part
+
         return carry
 
-    lax.fori_loop(0, tiles, one, 0)
+    lax.fori_loop(0, comps, one, 0)
     hit = total[nvar * pairs :, :] > 0.5
     for v in range(nvar):
         out_ref[v] = jnp.where(hit, total[v * pairs : (v + 1) * pairs, :], state_ref[v])
+    for d in range(1, comps):
+        copy(d).wait_send()
 
 
 def scatter(state, cells, values):
     nvar, rows, width_y, width_z = state.shape
     pairs = rows * width_y
-    tile = cells.shape[2]
+    comps, slots, _, tile = cells.shape
     vmem = pl.BlockSpec(memory_space=pltpu.VMEM)
     out = pl.pallas_call(
-        functools.partial(scatter_kernel, width_z.bit_length() - 1),
+        functools.partial(scatter_kernel, comps, width_z.bit_length() - 1),
         out_shape=jax.ShapeDtypeStruct((nvar, pairs, width_z), F32),
         in_specs=[vmem] * 3,
         out_specs=vmem,
         scratch_shapes=[
-            pltpu.VMEM(((nvar + 1) * pairs, 2 * tile), BF16),
+            pltpu.VMEM(((nvar + 1) * pairs, 2 * slots * tile), BF16),
             pltpu.VMEM(((nvar + 1) * pairs, width_z), F32),
+            pltpu.VMEM(values.shape, F32),
+            pltpu.SemaphoreType.DMA((comps,)),
+            pltpu.SemaphoreType.DMA((comps,)),
         ],
-        compiler_params=pltpu.CompilerParams(vmem_limit_bytes=VMEM_LIMIT),
+        compiler_params=pltpu.CompilerParams(
+            collective_id=2, has_side_effects=True, vmem_limit_bytes=VMEM_LIMIT
+        ),
         name="scatter",
     )(state.reshape(nvar, pairs, width_z), cells, values)
     return out.reshape(state.shape)
@@ -320,19 +409,17 @@
     slot = jnp.arange(slots, dtype=jnp.int32)[None, :]
     live_in = lax.dynamic_index_in_dim(pair_tiles[0], mine, 1, keepdims=False)
     live_out = lax.dynamic_index_in_dim(pair_tiles[0], mine, 0, keepdims=False)
-    keep = (slot < live_in[:, None]).reshape(tiles, 1, 1)
-    cells = jnp.where(keep, recv_cell[0, 0].reshape(tiles, 1, tile), -1)
+    keep = (slot < live_in[:, None]).reshape(comps, slots, 1, 1)
+    cells = jnp.where(keep, recv_cell[0, 0].reshape(comps, slots, 1, tile), -1)
     send = (slot < live_out[:, None]).astype(jnp.int32).reshape(tiles)
     base = donor_cell[0, 0].reshape(tiles, corners, tile)[:, :1]
-    held = lax.all_to_all(interp_weight[0, 0], "comp", split_axis=0, concat_axis=0, tiled=True)
+    state, held = relax(jac, now, now, prev, kappa, interp_weight[0, 0])
     held = held.reshape(tiles, corners, tile)
-    state = now
     for sub in range(SUBITERS):
-        state = relax(jac, state, now, prev, kappa)
+        if sub > 0:
+            (state,) = relax(jac, state, now, prev, kappa)
         packed = gather(send, state, base, held)
-        packed = packed.reshape(comps, slots * nvar, tile)
-        arrived = lax.all_to_all(packed, "comp", split_axis=0, concat_axis=0, tiled=True)
-        state = scatter(state, cells, arrived.reshape(tiles, nvar, tile))
+        state = scatter(state, cells, packed.reshape(comps, slots, nvar, tile))
     return state[None]
 
 

time: 138 us -> 124 us (0.90)
  Pallas kernels: 104 us -> 115 us
  starting transfers between devices: 9.92 us -> 0 us
  blocking collectives: 8.61 us -> 0 us
  waiting for transfers between devices: 5.24 us -> 0 us
    pallas_call x4, Pallas kernels: 88.6 us -> 98.9 us  [the longest x2 70.7 us: relax(): pl.pallas_call(functools.partial(relax_kernel, count, comps), out_shape=o...]
    all_to_all x2 -> x0, starting transfers between devices: 9.92 us -> none  [the longest x1 5.01 us: shards(): lax.all_to_all(interp_weight[0, 0], 'comp', split_axis=0, concat_axis=0,...]
    all_to_all x1 -> x0, blocking collectives: 8.61 us -> none  [shards(): lax.all_to_all(packed, 'comp', split_axis=0, concat_axis=0, tiled=True)]
    all_to_all x2 -> x0, waiting for transfers between devices: 5.24 us -> none  [the longest x1 5.23 us: shards(): lax.all_to_all(packed, 'comp', split_axis=0, concat_axis=0, tiled=True)]
    reshape x4 -> x0, local copies, waits for them, and re-layouts: 3.57 us -> none  [the longest x2 2.31 us: shards(): packed = packed.reshape(comps, slots * nvar, tile)]
    unnamed x7 -> x4, local copies, waits for them, and re-layouts: 1.92 us -> 4.71 us
  transfers between devices with their start and end apart: 2 -> 0, of which waited for: 1 -> 0; matrix products, arithmetic and copies ran while one was open for 3% -> 0% of each run, Pallas kernels for 26% -> 0%
where the time goes in v1:
time: 124 us; the launch traced here: 123 us
  Pallas kernels  115 us (93%)
  local copies, waits for them, and re-layouts  6.93 us (6%)
  other arithmetic  1.51 us (1%)
    pallas_call x2, Pallas kernels, relax(): pl.pallas_call(functools.partial(relax_kernel, count, comps), out_shape=o...  70.7 us
    pallas_call x2, Pallas kernels, scatter(): pl.pallas_call(functools.partial(scatter_kernel, comps, width_z.bit_lengt...  28.2 us
    pallas_call x2, Pallas kernels, gather(): pl.pallas_call(functools.partial(gather_kernel, (width_y, width_z.bit_len...  15.7 us
    unnamed x4, local copies, waits for them, and re-layouts  4.71 us

profile of v1, /device:TPU:6, one launch (start us, length us, event | category | flops | bytes accessed | tf_op | source)
XLA Modules:
  0.0 123.0 jit_solution(11536084351225586856)
XLA Ops:
  0.0 0.0 copy-start
  0.0 0.7 copy-done
  0.7 0.2 dynamic-slice_reduce_fusion
  0.9 0.1 iota_compare_fusion.1
  1.0 0.1 fusion
  1.0 0.6 reshape.76.live_ref
  1.6 1.4 %broadcast_select_fusion.cell_ref = s32[8,2,1,128]{3,2,1,0:T(1,128)} fusion(s32[8,2,1,128]{3,2,1,0:T(1,128)} %bitcast.38, pred[8,2]{1,0:T(8,128)(4,1)S(1)} %iota_compare_fusion.1), kind=kLoop, calls=%fused_computation | loop fusion | flops 2048 | bytes 16400 | tf_op jit(solution)/shard_map/jit(_where)/select_n | solution.py:413
  3.0 1.4 %slice.4.base_ref = s32[16,1,128]{2,1,0:T(1,128)} slice(s32[16,8,128]{2,1,0:T(8,128)} %bitcast.39), slice={[0:16], [0:1], [0:128]} | slice | bytes 16384 | tf_op jit(solution)/shard_map/slice | solution.py:415
  4.4 1.3 %copy.11 = f32[1,3,6,6]{3,2,0,1:T(8,128)} copy(f32[1,3,6,6]{3,0,2,1:T(1,128)} %param.11) | data formatting | bytes 864
  5.7 38.0 %relax.2 = (f32[6,8,32,256]{3,2,1,0:T(8,128)}, f32[8,2,8,128]{3,2,1,0:T(8,128)}) custom-call(f32[3,6,6]{2,1,0:T(8,128)} %bitcast.35, f32[6,8,32,256]{3,2,1,0:T(8,128)} %bitcast.20, f32[6,8,32,256]{3,2,1,0:T(8,128)} %bitcast.21, f32[6,8,32,256]{3,2,1,0:T(8,128)} %bitcast.27, f32[8,32,256]{2,1,0:T(8,128)} %bitcast.29, f32[8,2,8,128]{3,2,1,0:T(8,128)} %bitcast.37), custom_call_target="tpu_custom_call" | custom-call | tf_op jit(solution)/shard_map/relax/pallas_call | solution.py:237
  43.8 7.8 %gather.2 = f32[16,6,128]{2,1,0:T(8,128)} custom-call(s32[16]{0:T(128)} %reshape.76.live_ref, f32[6,256,256]{2,1,0:T(8,128)} %bitcast.23, s32[16,1,128]{2,1,0:T(1,128)} %slice.4.base_ref, f32[16,8,128]{2,1,0:T(8,128)} %bitcast.31), custom_call_target="tpu_custom_call" | custom-call | tf_op jit(solution)/shard_map/gather/pallas_call | solution.py:296
  51.6 14.1 %scatter.2 = f32[6,256,256]{2,1,0:T(8,128)} custom-call(f32[6,256,256]{2,1,0:T(8,128)} %bitcast.24, s32[8,2,1,128]{3,2,1,0:T(1,128)} %broadcast_select_fusion.cell_ref, f32[8,2,6,128]{3,2,1,0:T(8,128)} %bitcast.34), custom_call_target="tpu_custom_call" | custom-call | tf_op jit(solution)/shard_map/scatter/pallas_call | solution.py:377
  65.7 32.7 %relax.3 = f32[6,8,32,256]{3,2,1,0:T(8,128)} custom-call(f32[3,6,6]{2,1,0:T(8,128)} %bitcast.36, f32[6,8,32,256]{3,2,1,0:T(8,128)} %bitcast.26, f32[6,8,32,256]{3,2,1,0:T(8,128)} %bitcast.22, f32[6,8,32,256]{3,2,1,0:T(8,128)} %bitcast.28, f32[8,32,256]{2,1,0:T(8,128)} %bitcast.30), custom_call_target="tpu_custom_call" | custom-call | tf_op jit(solution)/shard_map/relax/pallas_call | solution.py:237
  98.3 7.8 %gather.3 = f32[16,6,128]{2,1,0:T(8,128)} custom-call(s32[16]{0:T(128)} %reshape.76.live_ref, f32[6,256,256]{2,1,0:T(8,128)} %bitcast.18, s32[16,1,128]{2,1,0:T(1,128)} %slice.4.base_ref, f32[16,8,128]{2,1,0:T(8,128)} %bitcast.32), custom_call_target="tpu_custom_call" | custom-call | tf_op jit(solution)/shard_map/gather/pallas_call | solution.py:296
  106.2 14.1 %scatter.3 = f32[6,256,256]{2,1,0:T(8,128)} custom-call(f32[6,256,256]{2,1,0:T(8,128)} %bitcast.19, s32[8,2,1,128]{3,2,1,0:T(1,128)} %broadcast_select_fusion.cell_ref, f32[8,2,6,128]{3,2,1,0:T(8,128)} %bitcast.33), custom_call_target="tpu_custom_call" | custom-call | tf_op jit(solution)/shard_map/scatter/pallas_call | solution.py:377
  120.3 2.7 %copy.13 = f32[1,6,8,32,256]{4,3,2,1,0:T(8,128)} copy(f32[1,6,8,32,256]{4,3,2,1,0:T(8,128)} %bitcast.25) | data formatting | bytes 3145728
  (1 shorter events, 0.0 us)
Async XLA Ops:
  0.0 0.7 copy-start
